TPU v7x, 16 devices: a 4x2x1 block of a 4x4x8 slice. The times are simulated.
16 devices in a mesh: rep: 4 (over y, z, core), pp: 4 (over x).
Axes of the slice: x: 4, y: 2, z: 1, core: 2. Of those that a mesh axis runs over, the one named last changes fastest.
The devices are a block of a 4x4x8 slice.
Arguments:
- x: bfloat16 [32, 512, 512], P('rep'), parts along dimension 0
- dy: bfloat16 [32, 512, 512], P('rep'), parts along dimension 0
- w_gate: bfloat16 [4, 512, 1536], P('pp')
- w_up: bfloat16 [4, 512, 1536], P('pp')
- w_down: bfloat16 [4, 1536, 512], P('pp')
Outputs:
- output 1: bfloat16 [16, 512, 1536], P(('rep', 'pp')), parts along dimension 0
- output 2: bfloat16 [16, 512, 1536], P(('rep', 'pp')), parts along dimension 0
- output 3: bfloat16 [16, 1536, 512], P(('rep', 'pp')), parts along dimension 0
There are 4 independent parts. A program takes and returns all parts, laid end to end along the dimension named above; an argument that names none is the same for every part.
All inputs are finite; a program needn't handle non-finite values.
Results may differ from a plain program's by a relative error of at most 0.0181.
Values are sent between devices in bfloat16 or wider.
A program may use at most 768 MiB of HBM per device.

v0:
```python
import functools

import jax
import jax.numpy as jnp
from jax import lax
from jax.experimental import pallas as pl
from jax.experimental.pallas import tpu as pltpu
from jax.sharding import PartitionSpec as P

F32, BF16 = jnp.float32, jnp.bfloat16
ROWS = 128
LAG = 4
SLOTS = 14
RING = 6
LANES = 128


def dot(a, b):
    return jnp.dot(a, b, preferred_element_type=F32)


def dot_tokens(a, b):
    return lax.dot_general(a, b, (((0,), (0,)), ((), ())), preferred_element_type=F32)


def scale_of(wide):
    return lax.rsqrt(jnp.mean(wide * wide, -1, keepdims=True) + 1e-6)


def sigmoid(v):
    return 0.5 * jnp.tanh(0.5 * v) + 0.5


def transpose_down(wd, wdt):
    @pl.loop(0, wd.shape[0] // LANES)
    def _(i):
        part = pl.ds(pl.multiple_of(i * LANES, LANES), LANES)
        wdt[:, part] = wd[part, :].T


def transpose_gate_up(wgu, wgut):
    @pl.loop(0, wgu.shape[1] // LANES)
    def _(i):
        part = pl.ds(pl.multiple_of(i * LANES, LANES), LANES)
        wgut[part, :] = wgu[:, part].T


def forward_chunk(hc, wgu, wd, keep, onward, out):
    ff = wd.shape[0]
    wide = hc.astype(F32)
    a = (wide * scale_of(wide)).astype(BF16)
    if not onward:
        keep[...] = dot(a, wgu[...])
        return
    acts = []
    width = ff // 3
    for i in range(3):
        lo, hi = i * width, (i + 1) * width
        gate = dot(a, wgu[:, lo:hi])
        up = dot(a, wgu[:, ff + lo : ff + hi])
        keep[:, lo:hi] = gate
        keep[:, ff + lo : ff + hi] = up
        acts.append((gate * sigmoid(gate) * up).astype(BF16))
    act = jnp.concatenate(acts, axis=1)
    out[...] = hc + dot(act, wd[...]).astype(BF16)


def backward_chunk(hc, gc, wdt, wgut, keep, a_out, act_out, dgu_out, onward, out):
    ff = wdt.shape[1]
    wide = hc.astype(F32)
    scale = scale_of(wide)
    a_out[...] = (wide * scale).astype(BF16)
    gates, ups = [], []
    width = ff // 3
    for i in range(3):
        lo, hi = i * width, (i + 1) * width
        d = dot(gc, wdt[:, lo:hi]).astype(BF16).astype(F32)
        gate, up = keep[:, lo:hi], keep[:, ff + lo : ff + hi]
        sig = sigmoid(gate)
        silu = gate * sig
        act_out[:, lo:hi] = (silu * up).astype(BF16)
        by_up = (d * silu).astype(BF16)
        by_gate = (d * up * (sig + silu * (1.0 - sig))).astype(BF16)
        dgu_out[:, lo:hi] = by_gate
        dgu_out[:, ff + lo : ff + hi] = by_up
        gates.append(by_gate)
        ups.append(by_up)
    if not onward:
        return
    by_a = dot(jnp.concatenate(gates, axis=1), wgut[:ff, :]).astype(BF16) + dot(jnp.concatenate(ups, axis=1), wgut[ff:, :]).astype(BF16)
    by_a = by_a.astype(F32)
    inner = jnp.sum(by_a * wide, -1, keepdims=True) * (scale * scale * scale * (1.0 / wide.shape[-1]))
    out[...] = gc + (by_a * scale - wide * inner).astype(BF16)


def weight_terms(a, g, dgu, act):
    return dot_tokens(a, dgu).astype(BF16).astype(F32), dot_tokens(g, act).astype(BF16).astype(F32)


def kernel(
    stages,
    micro,
    tokens,
    x,
    dy,
    w_gate,
    w_up,
    w_down,
    o_gate,
    o_up,
    o_down,
    wgu,
    wd,
    wgut,
    wdt,
    h,
    g,
    hs,
    gs,
    keep,
    a_keep,
    act_keep,
    dgu_keep,
    acc_gu,
    acc_d,
    w_sem,
    o_sem,
    h_recv,
    g_recv,
    h_send,
    g_send,
):
    me = lax.axis_index("pp")
    first, last = me == 0, me == stages - 1
    ff = wd.shape[0]
    per = tokens // ROWS
    chunks = micro * per
    band = wgu.shape[0] // per
    lag = LAG * (stages - 1 - me)

    def rows_of(c):
        return pl.ds(pl.multiple_of(c * ROWS, ROWS), ROWS)

    def from_x(c):
        return pltpu.make_async_copy(x.at[rows_of(c)], h.at[rows_of(c)], h_recv.at[c])

    def from_dy(c):
        return pltpu.make_async_copy(dy.at[rows_of(c)], g.at[rows_of(c)], g_recv.at[c])

    def send_h(c):
        slot = lax.rem(c, RING)
        return pltpu.make_async_remote_copy(
            src_ref=hs.at[slot],
            dst_ref=h.at[rows_of(c)],
            send_sem=h_send.at[slot],
            recv_sem=h_recv.at[c],
            device_id={"pp": lax.rem(me + 1, stages)},
            device_id_type=pl.DeviceIdType.MESH,
        )

    def send_g(c):
        slot = lax.rem(c, RING)
        return pltpu.make_async_remote_copy(
            src_ref=gs.at[slot],
            dst_ref=g.at[rows_of(c)],
            send_sem=g_send.at[slot],
            recv_sem=g_recv.at[c],
            device_id={"pp": lax.rem(me + stages - 1, stages)},
            device_id_type=pl.DeviceIdType.MESH,
        )

    @pl.when(first)
    def _():
        from_x(0).start()

    loads = (
        pltpu.make_async_copy(w_gate, wgu.at[:, pl.ds(0, ff)], w_sem.at[0]),
        pltpu.make_async_copy(w_up, wgu.at[:, pl.ds(ff, ff)], w_sem.at[1]),
        pltpu.make_async_copy(w_down, wd, w_sem.at[2]),
    )
    for load in loads:
        load.start()

    barrier = pltpu.get_barrier_semaphore()
    for other in (lax.rem(me + 1, stages), lax.rem(me + stages - 1, stages)):
        pl.semaphore_signal(barrier, inc=1, device_id={"pp": other}, device_id_type=pl.DeviceIdType.MESH)

    @pl.when(first)
    def _():
        @pl.loop(1, chunks)
        def _(c):
            from_x(c).start()

    @pl.when(last)
    def _():
        @pl.loop(0, chunks)
        def _(c):
            from_dy(c).start()

    acc_gu[...] = jnp.zeros_like(acc_gu)
    acc_d[...] = jnp.zeros_like(acc_d)
    for load in loads:
        load.wait()

    @pl.when(jnp.logical_not(first))
    def _():
        transpose_gate_up(wgu, wgut)
        transpose_down(wd, wdt)

    pl.semaphore_wait(barrier, 2)

    def out_copies(j):
        slot = (micro - 2) % 2
        rows = pl.ds(pl.multiple_of(j * band, band), band)
        return (
            pltpu.make_async_copy(dgu_keep.at[slot, rows, pl.ds(0, ff)], o_gate.at[rows], o_sem.at[0, j]),
            pltpu.make_async_copy(dgu_keep.at[slot, rows, pl.ds(ff, ff)], o_up.at[rows], o_sem.at[1, j]),
            pltpu.make_async_copy(act_keep.at[slot, rows], o_down.at[rows], o_sem.at[2, j]),
        )

    @pl.loop(0, chunks + LAG * (stages - 1) + per - 1)
    def _(t):
        @pl.when(t < chunks)
        def _():
            c = t
            slot = lax.rem(c, SLOTS)

            @pl.when(first)
            def _():
                from_x(c).wait()

            @pl.when(jnp.logical_not(first))
            def _():
                send_h(c).wait_recv()

            @pl.when(last)
            def _():
                forward_chunk(h[rows_of(c), :], wgu, wd, keep.at[slot], False, None)

            @pl.when(jnp.logical_not(last))
            def _():
                @pl.when(c >= RING)
                def _():
                    send_h(c).wait_send()

                forward_chunk(h[rows_of(c), :], wgu, wd, keep.at[slot], True, hs.at[lax.rem(c, RING)])
                send_h(c).start()

        @pl.when(jnp.logical_and(first, t == 2))
        def _():
            transpose_down(wd, wdt)

        @pl.when(jnp.logical_and(t >= lag, t < chunks + lag))
        def _():
            c = t - lag
            slot, half = lax.rem(c, SLOTS), lax.rem(lax.div(c, per), 2)
            inside = rows_of(lax.rem(c, per))

            @pl.when(last)
            def _():
                from_dy(c).wait()

            @pl.when(jnp.logical_not(last))
            def _():
                send_g(c).wait_recv()

            parts = (
                h[rows_of(c), :],
                g[rows_of(c), :],
                wdt,
                wgut,
                keep.at[slot],
                a_keep.at[half, inside],
                act_keep.at[half, inside],
                dgu_keep.at[half, inside],
            )

            @pl.when(first)
            def _():
                backward_chunk(*parts, False, None)

            @pl.when(jnp.logical_not(first))
            def _():
                @pl.when(c >= RING)
                def _():
                    send_g(c).wait_send()

                backward_chunk(*parts, True, gs.at[lax.rem(c, RING)])
                send_g(c).start()

        u = t - lag - (per - 1)

        @pl.when(jnp.logical_and(u >= 0, u < chunks))
        def _():
            m, j = lax.div(u, per), lax.rem(u, per)
            half = lax.rem(m, 2)
            rows = pl.ds(pl.multiple_of(j * band, band), band)
            by_gu, by_d = weight_terms(
                a_keep[half, :, rows],
                g[pl.ds(pl.multiple_of(m * tokens, tokens), tokens), rows],
                dgu_keep[half],
                act_keep[half],
            )

            @pl.when(m < micro - 1)
            def _():
                acc_gu[rows, :] += by_gu
                acc_d[rows, :] += by_d

            @pl.when(m == micro - 1)
            def _():
                other = (micro - 2) % 2
                dgu_keep[other, rows, :] = (acc_gu[rows, :] + by_gu).astype(BF16)
                act_keep[other, rows, :] = (acc_d[rows, :] + by_d).astype(BF16)
                for copy in out_copies(j):
                    copy.start()

    @pl.loop(0, min(RING, chunks))
    def _(c):
        @pl.when(jnp.logical_not(last))
        def _():
            send_h(c).wait_send()

        @pl.when(jnp.logical_not(first))
        def _():
            send_g(c).wait_send()

    @pl.loop(0, per)
    def _(j):
        for copy in out_copies(j):
            copy.wait()


def solution(mesh):
    stages = mesh.shape["pp"]

    def step(x, dy, w_gate, w_up, w_down):
        micro, tokens, d = x.shape
        ff = w_gate.shape[-1]
        assert w_gate.shape[0] == 1
        per = tokens // ROWS
        chunks = micro * per
        anywhere = pl.BlockSpec(memory_space=pl.ANY)
        tall = jax.ShapeDtypeStruct((d, ff), BF16)
        by_gate, by_up, by_down = pl.pallas_call(
            functools.partial(kernel, stages, micro, tokens),
            out_shape=(tall, tall, tall),
            in_specs=[anywhere] * 5,
            out_specs=(anywhere,) * 3,
            scratch_shapes=[
                pltpu.VMEM((d, 2 * ff), BF16),
                pltpu.VMEM((ff, d), BF16),
                pltpu.VMEM((2 * ff, d), BF16),
                pltpu.VMEM((d, ff), BF16),
                pltpu.VMEM((micro * tokens, d), BF16),
                pltpu.VMEM((micro * tokens, d), BF16),
                pltpu.VMEM((RING, ROWS, d), BF16),
                pltpu.VMEM((RING, ROWS, d), BF16),
                pltpu.VMEM((SLOTS, ROWS, 2 * ff), F32),
                pltpu.VMEM((2, tokens, d), BF16),
                pltpu.VMEM((2, tokens, ff), BF16),
                pltpu.VMEM((2, tokens, 2 * ff), BF16),
                pltpu.VMEM((d, 2 * ff), F32),
                pltpu.VMEM((d, ff), F32),
                pltpu.SemaphoreType.DMA((3,)),
                pltpu.SemaphoreType.DMA((3, per)),
                pltpu.SemaphoreType.DMA((chunks,)),
                pltpu.SemaphoreType.DMA((chunks,)),
                pltpu.SemaphoreType.DMA((RING,)),
                pltpu.SemaphoreType.DMA((RING,)),
            ],
            compiler_params=pltpu.CompilerParams(collective_id=0, has_side_effects=True, vmem_limit_bytes=67043328),
        )(x.reshape(micro * tokens, d), dy.reshape(micro * tokens, d), w_gate[0], w_up[0], w_down[0])
        return by_gate[None], by_up[None], by_down.T[None]

    return jax.shard_map(
        step,
        mesh=mesh,
        in_specs=(P("rep", None, None),) * 2 + (P("pp", None, None),) * 3,
        out_specs=(P(("rep", "pp"), None, None),) * 3,
        check_vma=False,
    )
```

profile of v0, /device:TPU:112, one launch (start us, length us, event | category | flops | bytes accessed | tf_op | source)
XLA Modules:
  0.0 145.5 jit_solution(3259908444327412809)
XLA Ops:
  0.6 139.0 %shard_map.76 = (bf16[512,1536]{1,0:T(8,128)(2,1)}, bf16[512,1536]{1,0:T(8,128)(2,1)}, bf16[512,1536]{1,0:T(8,128)(2,1)}) custom-call(bf16[4096,512]{1,0:T(8,128)(2,1)} %bitcast.10, bf16[4096,512]{1,0:T(8,128)(2,1)} %bitcast.11, bf16[512,1536]{1,0:T(8,128)(2,1)} %bitcast.12, bf16[512,1536]{1,0:T(8,128)(2,1)} %bitcast.13, bf16[1536,512]{1,0:T(8,128)(2,1)} %bitcast.14), custom_call_target="tpu_custom_call" | custom-call | tf_op jit(solution)/shard_map/pallas_call | solution.py:345
  139.6 0.0 copy-start.1
  139.7 2.7 %copy.8 = bf16[1,1536,512]{2,1,0:T(8,128)(2,1)} copy(bf16[1,1536,512]{1,2,0:T(8,128)(2,1)} %bitcast.17) | data formatting | bytes 3145728
  142.4 0.0 copy-done.1
  142.4 0.0 copy-start
  142.4 1.1 copy.11
  143.5 0.8 copy-done
  144.3 1.1 copy.12
Async XLA Ops:
  139.6 2.7 %copy-start.1 = (bf16[512,1536]{1,0:T(8,128)(2,1)S(1)}, bf16[512,1536]{1,0:T(8,128)(2,1)}, u32[]{:S(2)}) copy-start(bf16[512,1536]{1,0:T(8,128)(2,1)} %get-tuple-element.6) | copy-start | bytes 4718596
  142.4 2.0 %copy-start = (bf16[512,1536]{1,0:T(8,128)(2,1)S(1)}, bf16[512,1536]{1,0:T(8,128)(2,1)}, u32[]{:S(2)}) copy-start(bf16[512,1536]{1,0:T(8,128)(2,1)} %get-tuple-element.7) | copy-start | bytes 4718596
where the time goes:
time: 146 us; the launch traced here: 145 us
  Pallas kernels  139 us (95%)
  local copies, waits for them, and re-layouts  5.83 us (4%)
    pallas_call x1, Pallas kernels, step(): pl.pallas_call(functools.partial(kernel, stages, micro, tokens), out_shap...  139 us
    unnamed x7, local copies, waits for them, and re-layouts  5.83 us

commit v1 on v0

--- a/solution.py
+++ b/solution.py
@@ -9,9 +9,9 @@
 
 F32, BF16 = jnp.float32, jnp.bfloat16
 ROWS = 128
-LAG = 4
-SLOTS = 14
-RING = 6
+LAGS = (0, 4, 8, 12)
+SLOTS = max(LAGS) + 1
+RING = 5
 LANES = 128
 
 
@@ -45,27 +45,28 @@
         wgut[part, :] = wgu[:, part].T
 
 
-def forward_chunk(hc, wgu, wd, keep, onward, out):
+def forward_chunk(hc, wgu, wd, keep, act_out, out):
     ff = wd.shape[0]
     wide = hc.astype(F32)
     a = (wide * scale_of(wide)).astype(BF16)
-    if not onward:
-        keep[...] = dot(a, wgu[...])
-        return
     acts = []
-    width = ff // 3
-    for i in range(3):
+    width = ff // 6
+    for i in range(6):
         lo, hi = i * width, (i + 1) * width
         gate = dot(a, wgu[:, lo:hi])
         up = dot(a, wgu[:, ff + lo : ff + hi])
-        keep[:, lo:hi] = gate
-        keep[:, ff + lo : ff + hi] = up
-        acts.append((gate * sigmoid(gate) * up).astype(BF16))
-    act = jnp.concatenate(acts, axis=1)
-    out[...] = hc + dot(act, wd[...]).astype(BF16)
-
-
-def backward_chunk(hc, gc, wdt, wgut, keep, a_out, act_out, dgu_out, onward, out):
+        sig = sigmoid(gate)
+        silu = gate * sig
+        act = (silu * up).astype(BF16)
+        act_out[:, lo:hi] = act
+        keep[:, lo:hi] = up * (sig + silu * (1.0 - sig))
+        keep[:, ff + lo : ff + hi] = silu
+        acts.append(act)
+    if out is not None:
+        out[...] = hc + dot(jnp.concatenate(acts, axis=1), wd[...]).astype(BF16)
+
+
+def backward_chunk(hc, gc, wdt, wgut, keep, a_out, dgu_out, out):
     ff = wdt.shape[1]
     wide = hc.astype(F32)
     scale = scale_of(wide)
@@ -75,17 +76,13 @@
     for i in range(3):
         lo, hi = i * width, (i + 1) * width
         d = dot(gc, wdt[:, lo:hi]).astype(BF16).astype(F32)
-        gate, up = keep[:, lo:hi], keep[:, ff + lo : ff + hi]
-        sig = sigmoid(gate)
-        silu = gate * sig
-        act_out[:, lo:hi] = (silu * up).astype(BF16)
-        by_up = (d * silu).astype(BF16)
-        by_gate = (d * up * (sig + silu * (1.0 - sig))).astype(BF16)
+        by_gate = (d * keep[:, lo:hi]).astype(BF16)
+        by_up = (d * keep[:, ff + lo : ff + hi]).astype(BF16)
         dgu_out[:, lo:hi] = by_gate
         dgu_out[:, ff + lo : ff + hi] = by_up
         gates.append(by_gate)
         ups.append(by_up)
-    if not onward:
+    if out is None:
         return
     by_a = dot(jnp.concatenate(gates, axis=1), wgut[:ff, :]).astype(BF16) + dot(jnp.concatenate(ups, axis=1), wgut[ff:, :]).astype(BF16)
     by_a = by_a.astype(F32)
@@ -94,7 +91,7 @@
 
 
 def weight_terms(a, g, dgu, act):
-    return dot_tokens(a, dgu).astype(BF16).astype(F32), dot_tokens(g, act).astype(BF16).astype(F32)
+    return dot_tokens(a, dgu).astype(BF16).astype(F32), dot_tokens(act, g).astype(BF16).astype(F32)
 
 
 def kernel(
@@ -135,8 +132,12 @@
     ff = wd.shape[0]
     per = tokens // ROWS
     chunks = micro * per
-    band = wgu.shape[0] // per
-    lag = LAG * (stages - 1 - me)
+    d = wgu.shape[0]
+    band, tall = d // per, ff // per
+    pieces = ff // d
+    behind = stages - 1 - me
+    lag = sum(jnp.where(behind == i, LAGS[i], 0) for i in range(stages))
+    blocks = act_keep.shape[0]
 
     def rows_of(c):
         return pl.ds(pl.multiple_of(c * ROWS, ROWS), ROWS)
@@ -197,13 +198,16 @@
         def _(c):
             from_dy(c).start()
 
-    acc_gu[...] = jnp.zeros_like(acc_gu)
-    acc_d[...] = jnp.zeros_like(acc_d)
+    def clear():
+        acc_gu[...] = jnp.zeros_like(acc_gu)
+        acc_d[...] = jnp.zeros_like(acc_d)
+
     for load in loads:
         load.wait()
 
     @pl.when(jnp.logical_not(first))
     def _():
+        clear()
         transpose_gate_up(wgu, wgut)
         transpose_down(wd, wdt)
 
@@ -215,15 +219,22 @@
         return (
             pltpu.make_async_copy(dgu_keep.at[slot, rows, pl.ds(0, ff)], o_gate.at[rows], o_sem.at[0, j]),
             pltpu.make_async_copy(dgu_keep.at[slot, rows, pl.ds(ff, ff)], o_up.at[rows], o_sem.at[1, j]),
-            pltpu.make_async_copy(act_keep.at[slot, rows], o_down.at[rows], o_sem.at[2, j]),
+        ) + tuple(
+            pltpu.make_async_copy(
+                act_keep.at[(micro - 2) % blocks, rows, pl.ds(i * d, d)],
+                o_down.at[pl.ds(pl.multiple_of(j * tall + i * band, band), band)],
+                o_sem.at[2 + i, j],
+            )
+            for i in range(pieces)
         )
 
-    @pl.loop(0, chunks + LAG * (stages - 1) + per - 1)
+    @pl.loop(0, chunks + LAGS[stages - 1] + per - 1)
     def _(t):
         @pl.when(t < chunks)
         def _():
             c = t
             slot = lax.rem(c, SLOTS)
+            act_out = act_keep.at[lax.rem(lax.div(c, per), blocks), rows_of(lax.rem(c, per))]
 
             @pl.when(first)
             def _():
@@ -235,7 +246,7 @@
 
             @pl.when(last)
             def _():
-                forward_chunk(h[rows_of(c), :], wgu, wd, keep.at[slot], False, None)
+                forward_chunk(h[rows_of(c), :], wgu, wd, keep.at[slot], act_out, None)
 
             @pl.when(jnp.logical_not(last))
             def _():
@@ -243,12 +254,16 @@
                 def _():
                     send_h(c).wait_send()
 
-                forward_chunk(h[rows_of(c), :], wgu, wd, keep.at[slot], True, hs.at[lax.rem(c, RING)])
+                forward_chunk(h[rows_of(c), :], wgu, wd, keep.at[slot], act_out, hs.at[lax.rem(c, RING)])
                 send_h(c).start()
 
         @pl.when(jnp.logical_and(first, t == 2))
         def _():
             transpose_down(wd, wdt)
+
+        @pl.when(jnp.logical_and(first, t == 3))
+        def _():
+            clear()
 
         @pl.when(jnp.logical_and(t >= lag, t < chunks + lag))
         def _():
@@ -271,13 +286,12 @@
                 wgut,
                 keep.at[slot],
                 a_keep.at[half, inside],
-                act_keep.at[half, inside],
                 dgu_keep.at[half, inside],
             )
 
             @pl.when(first)
             def _():
-                backward_chunk(*parts, False, None)
+                backward_chunk(*parts, None)
 
             @pl.when(jnp.logical_not(first))
             def _():
@@ -285,7 +299,7 @@
                 def _():
                     send_g(c).wait_send()
 
-                backward_chunk(*parts, True, gs.at[lax.rem(c, RING)])
+                backward_chunk(*parts, gs.at[lax.rem(c, RING)])
                 send_g(c).start()
 
         u = t - lag - (per - 1)
@@ -295,23 +309,25 @@
             m, j = lax.div(u, per), lax.rem(u, per)
             half = lax.rem(m, 2)
             rows = pl.ds(pl.multiple_of(j * band, band), band)
+            tall_rows = pl.ds(pl.multiple_of(j * tall, tall), tall)
             by_gu, by_d = weight_terms(
                 a_keep[half, :, rows],
-                g[pl.ds(pl.multiple_of(m * tokens, tokens), tokens), rows],
+                g[pl.ds(pl.multiple_of(m * tokens, tokens), tokens), :],
                 dgu_keep[half],
-                act_keep[half],
+                act_keep[lax.rem(m, blocks), :, tall_rows],
             )
 
             @pl.when(m < micro - 1)
             def _():
                 acc_gu[rows, :] += by_gu
-                acc_d[rows, :] += by_d
+                acc_d[tall_rows, :] += by_d
 
             @pl.when(m == micro - 1)
             def _():
-                other = (micro - 2) % 2
-                dgu_keep[other, rows, :] = (acc_gu[rows, :] + by_gu).astype(BF16)
-                act_keep[other, rows, :] = (acc_d[rows, :] + by_d).astype(BF16)
+                dgu_keep[(micro - 2) % 2, rows, :] = (acc_gu[rows, :] + by_gu).astype(BF16)
+                total = (acc_d[tall_rows, :] + by_d).astype(BF16)
+                for i in range(pieces):
+                    act_keep[(micro - 2) % blocks, rows, i * d : (i + 1) * d] = total[i * band : (i + 1) * band, :]
                 for copy in out_copies(j):
                     copy.start()
 
@@ -329,6 +345,28 @@
     def _(j):
         for copy in out_copies(j):
             copy.wait()
+
+
+def hand_over(per, *refs):
+    ins, outs, held, sem = refs[:3], refs[3:6], refs[6:9], refs[9]
+    moves = []
+    for j in range(per):
+        for i in range(3):
+            size = ins[i].shape[0] // per
+            rows = pl.ds(j * size, size)
+            moves.append(
+                (
+                    pltpu.make_async_copy(ins[i].at[rows], held[i].at[0, rows], sem.at[0, i, j]),
+                    pltpu.make_async_copy(held[i].at[0, rows], outs[i].at[0, rows], sem.at[1, i, j]),
+                )
+            )
+    for take, _ in moves:
+        take.start()
+    for take, put in moves:
+        take.wait()
+        put.start()
+    for _, put in moves:
+        put.wait()
 
 
 def solution(mesh):
@@ -340,11 +378,12 @@
         assert w_gate.shape[0] == 1
         per = tokens // ROWS
         chunks = micro * per
+        blocks = pl.cdiv(LAGS[stages - 1] + 2 * per, per)
         anywhere = pl.BlockSpec(memory_space=pl.ANY)
         tall = jax.ShapeDtypeStruct((d, ff), BF16)
         by_gate, by_up, by_down = pl.pallas_call(
             functools.partial(kernel, stages, micro, tokens),
-            out_shape=(tall, tall, tall),
+            out_shape=(tall, tall, jax.ShapeDtypeStruct((ff, d), BF16)),
             in_specs=[anywhere] * 5,
             out_specs=(anywhere,) * 3,
             scratch_shapes=[
@@ -358,12 +397,12 @@
                 pltpu.VMEM((RING, ROWS, d), BF16),
                 pltpu.VMEM((SLOTS, ROWS, 2 * ff), F32),
                 pltpu.VMEM((2, tokens, d), BF16),
-                pltpu.VMEM((2, tokens, ff), BF16),
+                pltpu.VMEM((blocks, tokens, ff), BF16),
                 pltpu.VMEM((2, tokens, 2 * ff), BF16),
                 pltpu.VMEM((d, 2 * ff), F32),
-                pltpu.VMEM((d, ff), F32),
+                pltpu.VMEM((ff, d), F32),
                 pltpu.SemaphoreType.DMA((3,)),
-                pltpu.SemaphoreType.DMA((3, per)),
+                pltpu.SemaphoreType.DMA((2 + ff // d, per)),
                 pltpu.SemaphoreType.DMA((chunks,)),
                 pltpu.SemaphoreType.DMA((chunks,)),
                 pltpu.SemaphoreType.DMA((RING,)),
@@ -371,7 +410,14 @@
             ],
             compiler_params=pltpu.CompilerParams(collective_id=0, has_side_effects=True, vmem_limit_bytes=67043328),
         )(x.reshape(micro * tokens, d), dy.reshape(micro * tokens, d), w_gate[0], w_up[0], w_down[0])
-        return by_gate[None], by_up[None], by_down.T[None]
+        shapes = ((1, d, ff), (1, d, ff), (1, ff, d))
+        return pl.pallas_call(
+            functools.partial(hand_over, per),
+            out_shape=tuple(jax.ShapeDtypeStruct(shape, BF16) for shape in shapes),
+            in_specs=[anywhere] * 3,
+            out_specs=(anywhere,) * 3,
+            scratch_shapes=[pltpu.VMEM(shape, BF16) for shape in shapes] + [pltpu.SemaphoreType.DMA((2, 3, per))],
+        )(by_gate, by_up, by_down)
 
     return jax.shard_map(
         step,

time: 146 us -> 140 us (0.959)
  local copies, waits for them, and re-layouts: 5.83 us -> 0 us
    unnamed x7 -> x0, local copies, waits for them, and re-layouts: 5.83 us -> none
    pallas_call x0 -> x1, Pallas kernels: none -> 4.27 us  [step(): pl.pallas_call(functools.partial(hand_over, per), out_shape=tuple((jax.Sh...]
    pallas_call x1, Pallas kernels: 139 us -> 135 us  [step(): pl.pallas_call(functools.partial(kernel, stages, micro, tokens), out_shap...]
where the time goes in v1:
time: 140 us
  Pallas kernels  139 us (99%)
    pallas_call x1, Pallas kernels, step(): pl.pallas_call(functools.partial(kernel, stages, micro, tokens), out_shap...  135 us
    pallas_call x1, Pallas kernels, step(): pl.pallas_call(functools.partial(hand_over, per), out_shape=tuple((jax.Sh...  4.27 us

profile of v1, /device:TPU:112, one launch (start us, length us, event | category | flops | bytes accessed | tf_op | source)
XLA Modules:
  0.0 140.1 jit_solution(3836527443171335173)
XLA Ops:
  0.6 135.1 %shard_map.76 = (bf16[512,1536]{1,0:T(8,128)(2,1)}, bf16[512,1536]{1,0:T(8,128)(2,1)}, bf16[1536,512]{1,0:T(8,128)(2,1)}) custom-call(bf16[4096,512]{1,0:T(8,128)(2,1)} %bitcast.5, bf16[4096,512]{1,0:T(8,128)(2,1)} %bitcast.6, bf16[512,1536]{1,0:T(8,128)(2,1)} %bitcast.7, bf16[512,1536]{1,0:T(8,128)(2,1)} %bitcast.8, bf16[1536,512]{1,0:T(8,128)(2,1)} %bitcast.9), custom_call_target="tpu_custom_call" | custom-call | tf_op jit(solution)/shard_map/pallas_call | solution.py:384
  135.8 4.3 %shard_map.77 = (bf16[1,512,1536]{2,1,0:T(8,128)(2,1)}, bf16[1,512,1536]{2,1,0:T(8,128)(2,1)}, bf16[1,1536,512]{2,1,0:T(8,128)(2,1)}) custom-call(bf16[512,1536]{1,0:T(8,128)(2,1)} %get-tuple-element.6.refs_0_, bf16[512,1536]{1,0:T(8,128)(2,1)} %get-tuple-element.7.refs_1_, bf16[1536,512]{1,0:T(8,128)(2,1)} %get-tuple-element.8.refs_2_), custom_call_target="tpu_custom_call" | custom-call | tf_op jit(solution)/shard_map/pallas_call | solution.py:414

commit v2 on v1

--- a/solution.py
+++ b/solution.py
@@ -9,9 +9,9 @@
 
 F32, BF16 = jnp.float32, jnp.bfloat16
 ROWS = 128
-LAGS = (0, 4, 8, 12)
+LAGS = (0, 4, 8, 13)
 SLOTS = max(LAGS) + 1
-RING = 5
+RING = 3
 LANES = 128
 
 
@@ -70,7 +70,6 @@
     ff = wdt.shape[1]
     wide = hc.astype(F32)
     scale = scale_of(wide)
-    a_out[...] = (wide * scale).astype(BF16)
     gates, ups = [], []
     width = ff // 3
     for i in range(3):
@@ -82,16 +81,42 @@
         dgu_out[:, ff + lo : ff + hi] = by_up
         gates.append(by_gate)
         ups.append(by_up)
-    if out is None:
-        return
-    by_a = dot(jnp.concatenate(gates, axis=1), wgut[:ff, :]).astype(BF16) + dot(jnp.concatenate(ups, axis=1), wgut[ff:, :]).astype(BF16)
+    a_out[...] = (wide * scale).astype(BF16)
+    if out is not None:
+        send_back(gc, wide, scale, gates, ups, wgut, out)
+
+
+def both_ways_chunk(hc, gc, wgu, wdt, wgut, a_out, act_out, dgu_out, out):
+    ff = wdt.shape[1]
+    wide = hc.astype(F32)
+    scale = scale_of(wide)
+    a = (wide * scale).astype(BF16)
+    gates, ups = [], []
+    width = ff // 6
+    for i in range(6):
+        lo, hi = i * width, (i + 1) * width
+        gate = dot(a, wgu[:, lo:hi])
+        up = dot(a, wgu[:, ff + lo : ff + hi])
+        d = dot(gc, wdt[:, lo:hi]).astype(BF16).astype(F32)
+        sig = sigmoid(gate)
+        silu = gate * sig
+        act_out[:, lo:hi] = (silu * up).astype(BF16)
+        by_gate = (d * (up * (sig + silu * (1.0 - sig)))).astype(BF16)
+        by_up = (d * silu).astype(BF16)
+        dgu_out[:, lo:hi] = by_gate
+        dgu_out[:, ff + lo : ff + hi] = by_up
+        gates.append(by_gate)
+        ups.append(by_up)
+    a_out[...] = a
+    send_back(gc, wide, scale, gates, ups, wgut, out)
+
+
+def send_back(gc, wide, scale, gates, ups, wgut, out):
+    half = wgut.shape[0] // 2
+    by_a = dot(jnp.concatenate(gates, axis=1), wgut[:half, :]).astype(BF16) + dot(jnp.concatenate(ups, axis=1), wgut[half:, :]).astype(BF16)
     by_a = by_a.astype(F32)
     inner = jnp.sum(by_a * wide, -1, keepdims=True) * (scale * scale * scale * (1.0 / wide.shape[-1]))
     out[...] = gc + (by_a * scale - wide * inner).astype(BF16)
-
-
-def weight_terms(a, g, dgu, act):
-    return dot_tokens(a, dgu).astype(BF16).astype(F32), dot_tokens(act, g).astype(BF16).astype(F32)
 
 
 def kernel(
@@ -115,7 +140,6 @@
     hs,
     gs,
     keep,
-    a_keep,
     act_keep,
     dgu_keep,
     acc_gu,
@@ -213,6 +237,21 @@
 
     pl.semaphore_wait(barrier, 2)
 
+    early = tokens // 2
+
+    def spare(i):
+        return lax.rem(chunks + i, SLOTS)
+
+    def bands_of(j):
+        return pl.ds(pl.multiple_of(j * band, band), band), pl.ds(pl.multiple_of(j * tall, tall), tall)
+
+    def terms(m, j, start, size):
+        rows, tall_rows = bands_of(j)
+        of_all = pl.ds(pl.multiple_of(m * tokens + start, size), size)
+        part = pl.ds(start, size)
+        by_gu = dot_tokens(h[of_all, rows], dgu_keep[lax.rem(m, 2), part, :])
+        return by_gu, dot_tokens(act_keep[lax.rem(m, blocks), part, tall_rows], g[of_all, :])
+
     def out_copies(j):
         slot = (micro - 2) % 2
         rows = pl.ds(pl.multiple_of(j * band, band), band)
@@ -244,10 +283,6 @@
             def _():
                 send_h(c).wait_recv()
 
-            @pl.when(last)
-            def _():
-                forward_chunk(h[rows_of(c), :], wgu, wd, keep.at[slot], act_out, None)
-
             @pl.when(jnp.logical_not(last))
             def _():
                 @pl.when(c >= RING)
@@ -279,19 +314,13 @@
             def _():
                 send_g(c).wait_recv()
 
-            parts = (
-                h[rows_of(c), :],
-                g[rows_of(c), :],
-                wdt,
-                wgut,
-                keep.at[slot],
-                a_keep.at[half, inside],
-                dgu_keep.at[half, inside],
-            )
+            def backward(out):
+                rows = rows_of(c)
+                backward_chunk(h[rows, :], g[rows, :], wdt, wgut, keep.at[slot], h.at[rows], dgu_keep.at[half, inside], out)
 
             @pl.when(first)
             def _():
-                backward_chunk(*parts, None)
+                backward(None)
 
             @pl.when(jnp.logical_not(first))
             def _():
@@ -299,7 +328,17 @@
                 def _():
                     send_g(c).wait_send()
 
-                backward_chunk(*parts, gs.at[lax.rem(c, RING)])
+                back = gs.at[lax.rem(c, RING)]
+
+                @pl.when(last)
+                def _():
+                    act_out = act_keep.at[lax.rem(lax.div(c, per), blocks), inside]
+                    both_ways_chunk(h[rows_of(c), :], g[rows_of(c), :], wgu, wdt, wgut, h.at[rows_of(c)], act_out, dgu_keep.at[half, inside], back)
+
+                @pl.when(jnp.logical_not(last))
+                def _():
+                    backward(back)
+
                 send_g(c).start()
 
         u = t - lag - (per - 1)
@@ -307,29 +346,44 @@
         @pl.when(jnp.logical_and(u >= 0, u < chunks))
         def _():
             m, j = lax.div(u, per), lax.rem(u, per)
-            half = lax.rem(m, 2)
-            rows = pl.ds(pl.multiple_of(j * band, band), band)
-            tall_rows = pl.ds(pl.multiple_of(j * tall, tall), tall)
-            by_gu, by_d = weight_terms(
-                a_keep[half, :, rows],
-                g[pl.ds(pl.multiple_of(m * tokens, tokens), tokens), :],
-                dgu_keep[half],
-                act_keep[lax.rem(m, blocks), :, tall_rows],
-            )
-
-            @pl.when(m < micro - 1)
-            def _():
-                acc_gu[rows, :] += by_gu
-                acc_d[tall_rows, :] += by_d
-
-            @pl.when(m == micro - 1)
-            def _():
-                dgu_keep[(micro - 2) % 2, rows, :] = (acc_gu[rows, :] + by_gu).astype(BF16)
-                total = (acc_d[tall_rows, :] + by_d).astype(BF16)
+            final = m == micro - 1
+
+            def finish(by_gu, by_d):
+                rows, tall_rows = bands_of(j)
+                dgu_keep[(micro - 2) % 2, rows, :] = (acc_gu[rows, :] + by_gu.astype(BF16).astype(F32)).astype(BF16)
+                total = (acc_d[tall_rows, :] + by_d.astype(BF16).astype(F32)).astype(BF16)
                 for i in range(pieces):
                     act_keep[(micro - 2) % blocks, rows, i * d : (i + 1) * d] = total[i * band : (i + 1) * band, :]
                 for copy in out_copies(j):
                     copy.start()
+
+            @pl.when(jnp.logical_not(final))
+            def _():
+                rows, tall_rows = bands_of(j)
+                by_gu, by_d = terms(m, j, 0, tokens)
+                acc_gu[rows, :] += by_gu.astype(BF16).astype(F32)
+                acc_d[tall_rows, :] += by_d.astype(BF16).astype(F32)
+
+            @pl.when(jnp.logical_and(final, jnp.logical_not(first)))
+            def _():
+                finish(*terms(m, j, 0, tokens))
+
+            @pl.when(jnp.logical_and(final, first))
+            def _():
+                by_gu, by_d = terms(m, j, early, tokens - early)
+                held = keep[spare(2 * j + 1)]
+                part = jnp.concatenate([held[:, i * d : (i + 1) * d] for i in range(pieces)], axis=0)
+                finish(keep[spare(2 * j)] + by_gu, part + by_d)
+
+        e = u - (chunks - per) + per // 2
+
+        @pl.when(jnp.logical_and(first, jnp.logical_and(e >= 0, e < per // 2)))
+        def _():
+            for j in (2 * e, 2 * e + 1):
+                by_gu, by_d = terms(micro - 1, j, 0, early)
+                keep[spare(2 * j)] = by_gu
+                for i in range(pieces):
+                    keep[spare(2 * j + 1), :, i * d : (i + 1) * d] = by_d[i * band : (i + 1) * band, :]
 
     @pl.loop(0, min(RING, chunks))
     def _(c):
@@ -378,7 +432,7 @@
         assert w_gate.shape[0] == 1
         per = tokens // ROWS
         chunks = micro * per
-        blocks = pl.cdiv(LAGS[stages - 1] + 2 * per, per)
+        blocks = (LAGS[stages - 1] + 2 * per - 2) // per + 1
         anywhere = pl.BlockSpec(memory_space=pl.ANY)
         tall = jax.ShapeDtypeStruct((d, ff), BF16)
         by_gate, by_up, by_down = pl.pallas_call(
@@ -396,7 +450,6 @@
                 pltpu.VMEM((RING, ROWS, d), BF16),
                 pltpu.VMEM((RING, ROWS, d), BF16),
                 pltpu.VMEM((SLOTS, ROWS, 2 * ff), F32),
-                pltpu.VMEM((2, tokens, d), BF16),
                 pltpu.VMEM((blocks, tokens, ff), BF16),
                 pltpu.VMEM((2, tokens, 2 * ff), BF16),
                 pltpu.VMEM((d, 2 * ff), F32),

time: 140 us -> 136 us (0.971)
  Pallas kernels: 139 us -> 135 us
    pallas_call x1, Pallas kernels: 135 us -> 131 us  [step(): pl.pallas_call(functools.partial(kernel, stages, micro, tokens), out_shap...]
where the time goes in v2:
time: 136 us
  Pallas kernels  135 us (99%)
    pallas_call x1, Pallas kernels, step(): pl.pallas_call(functools.partial(kernel, stages, micro, tokens), out_shap...  131 us
    pallas_call x1, Pallas kernels, step(): pl.pallas_call(functools.partial(hand_over, per), out_shape=tuple((jax.Sh...  4.27 us

profile of v2, /device:TPU:112, one launch (start us, length us, event | category | flops | bytes accessed | tf_op | source)
XLA Modules:
  0.0 135.8 jit_solution(7559724056134712814)
XLA Ops:
  0.6 130.9 %shard_map.76 = (bf16[512,1536]{1,0:T(8,128)(2,1)}, bf16[512,1536]{1,0:T(8,128)(2,1)}, bf16[1536,512]{1,0:T(8,128)(2,1)}) custom-call(bf16[4096,512]{1,0:T(8,128)(2,1)} %bitcast.5, bf16[4096,512]{1,0:T(8,128)(2,1)} %bitcast.6, bf16[512,1536]{1,0:T(8,128)(2,1)} %bitcast.7, bf16[512,1536]{1,0:T(8,128)(2,1)} %bitcast.8, bf16[1536,512]{1,0:T(8,128)(2,1)} %bitcast.9), custom_call_target="tpu_custom_call" | custom-call | tf_op jit(solution)/shard_map/pallas_call | solution.py:438
  131.6 4.3 %shard_map.77 = (bf16[1,512,1536]{2,1,0:T(8,128)(2,1)}, bf16[1,512,1536]{2,1,0:T(8,128)(2,1)}, bf16[1,1536,512]{2,1,0:T(8,128)(2,1)}) custom-call(bf16[512,1536]{1,0:T(8,128)(2,1)} %get-tuple-element.6.refs_0_, bf16[512,1536]{1,0:T(8,128)(2,1)} %get-tuple-element.7.refs_1_, bf16[1536,512]{1,0:T(8,128)(2,1)} %get-tuple-element.8.refs_2_), custom_call_target="tpu_custom_call" | custom-call | tf_op jit(solution)/shard_map/pallas_call | solution.py:467

commit v3 on v2

--- a/solution.py
+++ b/solution.py
@@ -194,9 +194,12 @@
             device_id_type=pl.DeviceIdType.MESH,
         )
 
+    ahead = 2
+
     @pl.when(first)
     def _():
-        from_x(0).start()
+        for c in range(ahead):
+            from_x(c).start()
 
     loads = (
         pltpu.make_async_copy(w_gate, wgu.at[:, pl.ds(0, ff)], w_sem.at[0]),
@@ -210,9 +213,16 @@
     for other in (lax.rem(me + 1, stages), lax.rem(me + stages - 1, stages)):
         pl.semaphore_signal(barrier, inc=1, device_id={"pp": other}, device_id_type=pl.DeviceIdType.MESH)
 
+    def clear():
+        acc_gu[...] = jnp.zeros_like(acc_gu)
+        acc_d[...] = jnp.zeros_like(acc_d)
+
+    for load in loads:
+        load.wait()
+
     @pl.when(first)
     def _():
-        @pl.loop(1, chunks)
+        @pl.loop(ahead, chunks)
         def _(c):
             from_x(c).start()
 
@@ -221,13 +231,6 @@
         @pl.loop(0, chunks)
         def _(c):
             from_dy(c).start()
-
-    def clear():
-        acc_gu[...] = jnp.zeros_like(acc_gu)
-        acc_d[...] = jnp.zeros_like(acc_d)
-
-    for load in loads:
-        load.wait()
 
     @pl.when(jnp.logical_not(first))
     def _():
@@ -348,7 +351,7 @@
             m, j = lax.div(u, per), lax.rem(u, per)
             final = m == micro - 1
 
-            def finish(by_gu, by_d):
+            def finish(j, by_gu, by_d):
                 rows, tall_rows = bands_of(j)
                 dgu_keep[(micro - 2) % 2, rows, :] = (acc_gu[rows, :] + by_gu.astype(BF16).astype(F32)).astype(BF16)
                 total = (acc_d[tall_rows, :] + by_d.astype(BF16).astype(F32)).astype(BF16)
@@ -366,14 +369,15 @@
 
             @pl.when(jnp.logical_and(final, jnp.logical_not(first)))
             def _():
-                finish(*terms(m, j, 0, tokens))
-
-            @pl.when(jnp.logical_and(final, first))
-            def _():
-                by_gu, by_d = terms(m, j, early, tokens - early)
-                held = keep[spare(2 * j + 1)]
-                part = jnp.concatenate([held[:, i * d : (i + 1) * d] for i in range(pieces)], axis=0)
-                finish(keep[spare(2 * j)] + by_gu, part + by_d)
+                finish(j, *terms(m, j, 0, tokens))
+
+            @pl.when(jnp.logical_and(jnp.logical_and(final, first), j < per // 2))
+            def _():
+                for b in (2 * j, 2 * j + 1):
+                    by_gu, by_d = terms(m, b, early, tokens - early)
+                    held = keep[spare(2 * b + 1)]
+                    part = jnp.concatenate([held[:, i * d : (i + 1) * d] for i in range(pieces)], axis=0)
+                    finish(b, keep[spare(2 * b)] + by_gu, part + by_d)
 
         e = u - (chunks - per) + per // 2
 

time: 136 us -> 136 us (level)
  no operation moved by 1% of the time
where the time goes in v3:
time: 136 us
  Pallas kernels  135 us (99%)
    pallas_call x1, Pallas kernels, step(): pl.pallas_call(functools.partial(kernel, stages, micro, tokens), out_shap...  131 us
    pallas_call x1, Pallas kernels, step(): pl.pallas_call(functools.partial(hand_over, per), out_shape=tuple((jax.Sh...  4.27 us

profile of v3, /device:TPU:112, one launch (start us, length us, event | category | flops | bytes accessed | tf_op | source)
XLA Modules:
  0.0 135.7 jit_solution(13062737601120594657)
XLA Ops:
  0.6 130.7 %shard_map.76 = (bf16[512,1536]{1,0:T(8,128)(2,1)}, bf16[512,1536]{1,0:T(8,128)(2,1)}, bf16[1536,512]{1,0:T(8,128)(2,1)}) custom-call(bf16[4096,512]{1,0:T(8,128)(2,1)} %bitcast.5, bf16[4096,512]{1,0:T(8,128)(2,1)} %bitcast.6, bf16[512,1536]{1,0:T(8,128)(2,1)} %bitcast.7, bf16[512,1536]{1,0:T(8,128)(2,1)} %bitcast.8, bf16[1536,512]{1,0:T(8,128)(2,1)} %bitcast.9), custom_call_target="tpu_custom_call" | custom-call | tf_op jit(solution)/shard_map/pallas_call | solution.py:442
  131.4 4.3 %shard_map.77 = (bf16[1,512,1536]{2,1,0:T(8,128)(2,1)}, bf16[1,512,1536]{2,1,0:T(8,128)(2,1)}, bf16[1,1536,512]{2,1,0:T(8,128)(2,1)}) custom-call(bf16[512,1536]{1,0:T(8,128)(2,1)} %get-tuple-element.6.refs_0_, bf16[512,1536]{1,0:T(8,128)(2,1)} %get-tuple-element.7.refs_1_, bf16[1536,512]{1,0:T(8,128)(2,1)} %get-tuple-element.8.refs_2_), custom_call_target="tpu_custom_call" | custom-call | tf_op jit(solution)/shard_map/pallas_call | solution.py:471
